TPU v7x, 64 devices: a 2x2x8 block of a 4x4x8 slice. The times are simulated.
64 devices in a mesh: dp: 8 (over x, y, core), sp: 8 (over z).
Axes of the slice: x: 2, y: 2, z: 8, core: 2. Of those that a mesh axis runs over, the one named last changes fastest.
The devices are a block of a 4x4x8 slice.
Arguments:
- q: bfloat16 [256, 16, 128], P('dp'), parts along dimension 0
- k: bfloat16 [256, 2048, 16, 128], P('dp', 'sp'), parts along dimension 0
- v: bfloat16 [256, 2048, 16, 128], P('dp', 'sp'), parts along dimension 0
Outputs:
- q: bfloat16 [256, 16, 128], P('dp'), parts along dimension 0
There are 8 independent parts. A program takes and returns all parts, laid end to end along the dimension named above; each array names one.
All inputs are finite; a program needn't handle non-finite values.
Results may differ from a plain program's by a relative error of at most 0.012.
Values are sent between devices in bfloat16 or wider.
A program may use at most 768 MiB of HBM per device.

v0:
```python
import jax
import jax.numpy as jnp
from jax import lax
from jax.sharding import PartitionSpec as P


def einsum(form, a, b):
    return jnp.einsum(form, a.astype(jnp.float32), b.astype(jnp.float32))


def part_of(q, k, v):
    grouped = q.reshape(q.shape[0], k.shape[2], -1, q.shape[2])
    scores = einsum("bgsd,bugd->bgsu", grouped, k) * q.shape[2] ** -0.5
    high = jnp.max(scores, -1, keepdims=True)
    weights = jnp.exp(scores - high)
    seen = einsum("bgsu,bugd->bgsd", weights.astype(jnp.bfloat16), v)
    return jnp.concatenate([seen, jnp.sum(weights, -1, keepdims=True), high], -1)


def together(parts):
    seen, total, high = parts[..., :-2], parts[..., -2:-1], parts[..., -1:]
    scale = jnp.exp(high - jnp.max(high, 0))
    return (jnp.sum(seen * scale, 0) / jnp.sum(total * scale, 0)).astype(jnp.bfloat16)


def solution(mesh):
    def step(q, k, v):
        return together(lax.all_gather(part_of(q, k, v), "sp")).reshape(q.shape)

    return jax.shard_map(
        step,
        mesh=mesh,
        in_specs=(P("dp", None, None), P("dp", "sp", None, None), P("dp", "sp", None, None)),
        out_specs=P("dp", None, None),
        check_vma=False,
    )
```

profile of v0, /device:TPU:21, one launch (start us, length us, event | category | flops | bytes accessed | tf_op | source)
XLA Modules:
  0.0 118.2 jit_solution(16547925177106445733)
XLA Ops:
  6.5 0.0 all-gather.3.cloned.1.call-start
  6.6 18.1 %fusion.2 = f32[32,16,1,256]{3,2,1,0:T(1,128)S(1)} fusion(bf16[32,256,16,128]{3,2,1,0:T(8,128)(2,1)} %param.4, bf16[32,16,128,1]{2,1,0,3:T(8,128)(2,1)} %bitcast.24), kind=kOutput, calls=%fused_computation.2 | convolution fusion | flops 33554432 | bytes 34209792 | tf_op jit(solution)/shard_map/bgsd,bugd->bgsu/dot_general | solution.py:8
  24.7 0.1 fusion.9
  24.8 0.3 fusion.10
  25.1 0.3 copy.23
  25.3 0.3 copy.22
  25.6 19.2 %fusion = f32[32,16,1,128]{3,2,1,0:T(1,128)S(1)} fusion(bf16[32,256,16,128]{3,2,1,0:T(8,128)(2,1)} %param.5, bf16[32,16,256,1]{2,1,0,3:T(8,128)(2,1)S(1)} %get-tuple-element.7), kind=kOutput, calls=%fused_computation | convolution fusion | flops 33554432 | bytes 34078720 | tf_op jit(solution)/shard_map/bgsu,bugd->bgsd/dot_general | solution.py:8
  44.8 0.9 pad_maximum_fusion
  45.7 0.1 all-gather.3.cloned.1.call-update
  45.8 55.9 %all-gather.3.cloned.1.call-done = f32[256,16,1,130]{3,1,2,0:T(8,128)} async-done(((f32[32,16,1,130]{3,1,2,0:T(8,128)}), f32[256,16,1,130]{3,1,2,0:T(8,128)}) %all-gather.3.cloned.1.call-update) | async-done | bytes 2129936 | tf_op jit(solution)/shard_map/all_gather | solution.py:28
  101.7 2.3 %slice_reduce_fusion = f32[32,16]{1,0:T(8,128)S(1)} fusion(f32[8,32,16,1,130]{4,2,1,0,3:T(8,128)} %bitcast.21), kind=kLoop, calls=%fused_computation.9 | loop fusion | flops 3584 | bytes 18432 | tf_op jit(solution)/shard_map/reduce_max | solution.py:22
  104.0 3.0 %fusion.4 = (f32[32,16]{1,0:T(8,128)S(1)}, f32[8,32,16,1,1]{4,2,1,0,3:T(8,128)S(1)}) fusion(f32[8,32,16,1,130]{4,2,1,0,3:T(8,128)} %bitcast.22, f32[32,16]{1,0:T(8,128)S(1)} %slice_reduce_fusion), kind=kLoop, calls=%fused_computation.5 | loop fusion | flops 11776 | bytes 53248 | tf_op jit(solution)/shard_map/reduce_sum | solution.py:23
  107.0 1.6 %copy.36 = f32[8,32,16,1,1]{2,1,0,3,4:T(8,128)S(1)} copy(f32[8,32,16,1,1]{4,2,1,0,3:T(8,128)S(1)} %get-tuple-element.6) | data formatting | bytes 32768 | tf_op jit(solution)/shard_map/mul | solution.py:23
  108.6 2.0 %fusion.5 = f32[32,16,128]{2,1,0:T(8,128)S(1)} fusion(f32[8,32,16,1,130]{4,2,1,0,3:T(8,128)} %bitcast.23, f32[8,32,16]{2,1,0:T(8,128)S(1)} %bitcast.25), kind=kLoop, calls=%fused_computation.7 | loop fusion | flops 983040 | bytes 2375680 | tf_op jit(solution)/shard_map/reduce_sum | solution.py:23
  110.6 0.8 divide_convert_fusion
Async XLA Ops:
  6.5 95.2 %all-gather.3.cloned.1.call-start = ((), (), s32[]{:S(2)}) async-start(), calls=%async_computation | async-start | bytes 4718592 | tf_op jit(solution)/shard_map/all_gather | solution.py:28
Sparse Core Ops, SparseCore 0:
  45.9 55.7 all-gather.2
where the time goes:
time: 118 us
  waiting for transfers between devices  56 us (47%)
  matrix products  37.3 us (32%)
  between operations  13.5 us (11%)
  other arithmetic  9.43 us (8%)
  local copies, waits for them, and re-layouts  2.08 us (2%)
    all_gather x1, waiting for transfers between devices, step(): return together(lax.all_gather(part_of(q, k, v), 'sp')).reshape(q.shape)  55.9 us
    dot_general x2, matrix products, einsum(): return jnp.einsum(form, a.astype(jnp.float32), b.astype(jnp.float32))  37.3 us
    reduce_sum x1, other arithmetic, together(): jnp.sum(total * scale, 0)  2.99 us
  transfers between devices with their start and end apart: 1, of which 1 were waited for; matrix products, arithmetic and copies ran while one was open for 0% of the time, Pallas kernels for 0%

commit v1 on v0

v1 whole, which is shorter than its diff:
```python
import functools

import jax
import jax.numpy as jnp
from jax import lax
from jax.experimental import pallas as pl
from jax.experimental.pallas import tpu as pltpu
from jax.sharding import PartitionSpec as P

LOG2E = 1.4426950408889634
SLOTS = 12
LANES = 128
MESH = pl.DeviceIdType.MESH


def kernel(axis, devices, rounds, q_hbm, k_hbm, v_hbm, o_ref, *scratch):
    (qbuf, kbuf, vbuf, sbuf, hbuf, pbuf, part, stat, rpart, rstat, tpart, tstat, cols, obuf,
     qsem, ksem, vsem, psend, precv, ssend, srecv, tpsend, tprecv, tssend, tsrecv, gsend, grecv) = scratch
    n, heads, head = q_hbm.shape
    half = k_hbm.shape[2]
    chunks = half // LANES
    shared = rounds * devices
    me = lax.axis_index(axis)
    others = sorted(range(1, devices), key=lambda d: -min(d, devices - d))
    factor = head ** -0.5 * LOG2E

    def peer(d):
        return lax.rem(me + d, devices)

    def to(src, dst, send, recv, device):
        return pltpu.make_async_remote_copy(src, dst, send, recv, device_id={axis: device}, device_id_type=MESH)

    def await_bytes(ref, sem):
        pltpu.make_async_copy(ref, ref, sem).wait()

    def kcopy(i):
        return pltpu.make_async_copy(k_hbm.at[i], kbuf.at[lax.rem(i, SLOTS)], ksem.at[lax.rem(i, SLOTS)])

    def vcopy(i):
        return pltpu.make_async_copy(v_hbm.at[i], vbuf.at[lax.rem(i, SLOTS)], vsem.at[lax.rem(i, SLOTS)])

    row = lax.broadcasted_iota(jnp.int32, (2 * heads, LANES), 0)
    lane = lax.broadcasted_iota(jnp.int32, (2 * heads, LANES), 1)
    keep = lax.rem(row, heads) == lax.rem(lane, heads)
    own = keep[:heads]
    first = row[:heads] == lane[:heads]

    def scores(i):
        q = qbuf[i]
        z = jnp.zeros_like(q)
        qq = jnp.concatenate([jnp.concatenate([q, z], 1), jnp.concatenate([z, q], 1)], 0)
        slot = lax.rem(i, SLOTS)
        kk = jnp.concatenate([kbuf[slot, 0], kbuf[slot, 1]], 1)
        s = lax.dot_general(qq, kk, (((1,), (1,)), ((), ())), preferred_element_type=jnp.float32)
        cs = [jnp.where(keep, s[:, c * LANES:(c + 1) * LANES], -jnp.inf) for c in range(chunks)]
        high = functools.reduce(jnp.maximum, cs)
        return cs, jnp.maximum(high[:heads], high[heads:])

    def put_scores(cs, high):
        for c in range(chunks):
            sbuf[:, c * LANES:(c + 1) * LANES] = cs[c]
        hbuf[...] = high

    def weigh():
        high = jnp.max(hbuf[...], 1, keepdims=True) * factor
        both = jnp.broadcast_to(jnp.concatenate([high, high], 0), (2 * heads, LANES))
        ps = [jnp.exp2(sbuf[:, c * LANES:(c + 1) * LANES] * factor - both) for c in range(chunks)]
        total = functools.reduce(jnp.add, ps)
        total = jnp.sum(total[:heads] + total[heads:], 1, keepdims=True)
        as_row = lambda x: jnp.sum(jnp.where(own, jnp.broadcast_to(x, (heads, LANES)), 0.0), 0, keepdims=True)
        return [p.astype(jnp.bfloat16) for p in ps], jnp.concatenate([as_row(high), as_row(total)], 0)

    def put_weights(ps):
        for c in range(chunks):
            pbuf[:, c * LANES:(c + 1) * LANES] = ps[c]

    def seen(i):
        slot = lax.rem(i, SLOTS)
        vv = jnp.concatenate([vbuf[slot, 0], vbuf[slot, 1]], 1)
        o = jnp.dot(pbuf[...], vv, preferred_element_type=jnp.float32)
        return (o[:heads, :head] + o[heads:, head:]).astype(jnp.bfloat16)

    def step(i, put_stat, put_part):
        kcopy(i + 2).wait()
        vcopy(i).wait()
        cs, high = scores(i + 2)
        ps, st = weigh()
        put_part(i, seen(i))
        put_stat(i + 1, st)
        put_scores(cs, high)
        put_weights(ps)

        @pl.when(i + 2 + SLOTS < n)
        def _():
            kcopy(i + 2 + SLOTS).start()

        @pl.when(i + SLOTS < n)
        def _():
            vcopy(i + SLOTS).start()

    def put_stat(i, st):
        stat[i] = st

    def put_part(i, x):
        part[i] = x

    def put_tail_stat(i, st):
        tstat[i - shared, me] = st

    def put_tail_part(i, x):
        tpart[i - shared, me] = x

    def send_round(g):
        for d in others:
            p = peer(d)
            to(stat.at[g * devices + p], rstat.at[g, me], ssend.at[g], srecv.at[g], p).start()
            to(part.at[g * devices + p], rpart.at[g, me], psend.at[g], precv.at[g], p).start()
        rstat[g, me] = stat[g * devices + me]
        rpart[g, me] = part[g * devices + me]

    def shares(st):
        high, total = st[:, 0, :], st[:, 1, :]
        e = jnp.exp2(high - jnp.max(high, 0, keepdims=True))
        w = e / jnp.sum(e * total, 0, keepdims=True)
        return [jnp.sum(jnp.where(first, jnp.broadcast_to(w[d:d + 1], (heads, LANES)), 0.0), 1, keepdims=True) for d in range(devices)]

    def join_round(g):
        await_bytes(rstat.at[g, pl.ds(0, devices - 1)], srecv.at[g])
        await_bytes(rpart.at[g, pl.ds(0, devices - 1)], precv.at[g])
        w = shares(rstat[g])
        i = g * devices + me
        obuf[i] = functools.reduce(jnp.add, [rpart[g, d].astype(jnp.float32) * w[d] for d in range(devices)]).astype(jnp.bfloat16)
        for d in others:
            to(obuf.at[i], obuf.at[i], gsend.at[g], grecv.at[g], peer(d)).start()

    def send_tail_stat(i):
        t = i - shared
        for d in others:
            to(tstat.at[t, me], tstat.at[t, me], tssend.at[t], tsrecv.at[t], peer(d)).start()

    def send_tail_part(i):
        t = i - shared
        for d in others:
            to(tpart.at[t, me], tpart.at[t, me], tpsend.at[t], tprecv.at[t], peer(d)).start()

    qcopy = pltpu.make_async_copy(q_hbm, qbuf, qsem)
    qcopy.start()
    kcopy(0).start()
    kcopy(1).start()

    @pl.loop(0, SLOTS - 2)
    def _(i):
        kcopy(i + 2).start()
        vcopy(i).start()

    vcopy(SLOTS - 2).start()
    vcopy(SLOTS - 1).start()
    barrier = pltpu.get_barrier_semaphore()
    for d in others:
        pl.semaphore_signal(barrier, inc=1, device_id={axis: peer(d)}, device_id_type=MESH)
    qcopy.wait()
    kcopy(0).wait()
    put_scores(*scores(0))
    kcopy(1).wait()
    cs, high = scores(1)
    ps, st = weigh()
    put_stat(0, st)
    put_scores(cs, high)
    put_weights(ps)
    kcopy(SLOTS).start()
    kcopy(SLOTS + 1).start()

    for g in range(rounds):
        last = g == rounds - 1

        @pl.loop(g * devices, (g + 1) * devices - last)
        def _(i):
            step(i, put_stat, put_part)

        if last:
            step(shared - 1, put_tail_stat, put_part)
        if g == 0:
            pl.semaphore_wait(barrier, devices - 1)
        send_round(g)
        if g:
            join_round(g - 1)

    send_tail_stat(shared)

    @pl.loop(shared, n - 2)
    def _(i):
        step(i, put_tail_stat, put_tail_part)
        send_tail_stat(i + 1)
        send_tail_part(i)

    vcopy(n - 2).wait()
    ps, st = weigh()
    put_tail_stat(n - 1, st)
    put_tail_part(n - 2, seen(n - 2))
    put_weights(ps)
    send_tail_stat(n - 1)
    send_tail_part(n - 2)
    join_round(rounds - 1)
    vcopy(n - 1).wait()
    put_tail_part(n - 1, seen(n - 1))
    send_tail_part(n - 1)

    @pl.loop(0, n - shared)
    def _(t):
        await_bytes(tstat.at[t, pl.ds(0, devices - 1)], tsrecv.at[t])
        w = shares(tstat[t])
        for d in range(devices):
            cols[t, d] = jnp.broadcast_to(w[d], (heads, head))

    @pl.loop(0, n - shared)
    def _(t):
        await_bytes(tpart.at[t, pl.ds(0, devices - 1)], tprecv.at[t])
        o_ref[shared + t] = functools.reduce(
            jnp.add, [tpart[t, d].astype(jnp.float32) * cols[t, d] for d in range(devices)]
        ).astype(jnp.bfloat16)

    for g in range(rounds):
        await_bytes(obuf.at[pl.ds(0, devices - 1)], grecv.at[g])
        await_bytes(obuf.at[pl.ds(0, devices - 1)], gsend.at[g])
        await_bytes(rstat.at[g, pl.ds(0, devices - 1)], ssend.at[g])
        await_bytes(rpart.at[g, pl.ds(0, devices - 1)], psend.at[g])
    for i in range(shared):
        o_ref[i] = obuf[i]

    @pl.loop(0, n - shared)
    def _(t):
        await_bytes(tstat.at[t, pl.ds(0, devices - 1)], tssend.at[t])
        await_bytes(tpart.at[t, pl.ds(0, devices - 1)], tpsend.at[t])


def attend(axis, devices, q, k, v):
    n, tokens, heads, head = k.shape
    half = tokens * heads // 2
    k = k.reshape(n, 2, half, head)
    v = v.reshape(n, 2, half, head)
    rounds = n // devices - 1
    shared = rounds * devices
    tail = n - shared
    dma = pltpu.SemaphoreType.DMA
    bf16, f32 = jnp.bfloat16, jnp.float32
    return pl.pallas_call(
        functools.partial(kernel, axis, devices, rounds),
        out_shape=jax.ShapeDtypeStruct((n, heads, head), bf16),
        in_specs=[pl.BlockSpec(memory_space=pl.ANY)] * 3,
        out_specs=pl.BlockSpec(memory_space=pltpu.VMEM),
        scratch_shapes=[
            pltpu.VMEM((n, heads, head), bf16),
            pltpu.VMEM((SLOTS, 2, half, head), bf16),
            pltpu.VMEM((SLOTS, 2, half, head), bf16),
            pltpu.VMEM((2 * heads, half), f32),
            pltpu.VMEM((heads, LANES), f32),
            pltpu.VMEM((2 * heads, half), bf16),
            pltpu.VMEM((shared, heads, head), bf16),
            pltpu.VMEM((shared, 2, LANES), f32),
            pltpu.VMEM((rounds, devices, heads, head), bf16),
            pltpu.VMEM((rounds, devices, 2, LANES), f32),
            pltpu.VMEM((tail, devices, heads, head), bf16),
            pltpu.VMEM((tail, devices, 2, LANES), f32),
            pltpu.VMEM((tail, devices, heads, head), f32),
            pltpu.VMEM((shared, heads, head), bf16),
            dma, dma((SLOTS,)), dma((SLOTS,)),
            dma((rounds,)), dma((rounds,)), dma((rounds,)), dma((rounds,)),
            dma((tail,)), dma((tail,)), dma((tail,)), dma((tail,)),
            dma((rounds,)), dma((rounds,)),
        ],
        compiler_params=pltpu.CompilerParams(collective_id=0, has_side_effects=True, vmem_limit_bytes=56 << 20),
        name="attend",
    )(q, k, v)


def solution(mesh):
    def step(q, k, v):
        return attend("sp", mesh.shape["sp"], q, k, v)

    return jax.shard_map(
        step,
        mesh=mesh,
        in_specs=(P("dp", None, None), P("dp", "sp", None, None), P("dp", "sp", None, None)),
        out_specs=P("dp", None, None),
        check_vma=False,
    )
```

time: 118 us -> 39 us (0.33)
  waiting for transfers between devices: 56 us -> 0 us
  matrix products: 37.3 us -> 0 us
  Pallas kernels: 0 us -> 37.3 us
  between operations: 13.5 us -> 0.01 us
  other arithmetic: 9.43 us -> 0 us
    all_gather x1 -> x0, waiting for transfers between devices: 55.9 us -> none  [step(): return together(lax.all_gather(part_of(q, k, v), 'sp')).reshape(q.shape)]
    pallas_call x0 -> x1, Pallas kernels: none -> 37.3 us  [attend(): pl.pallas_call(functools.partial(kernel, axis, devices, rounds), out_shap...]
    dot_general x2 -> x0, matrix products: 37.3 us -> none  [einsum(): return jnp.einsum(form, a.astype(jnp.float32), b.astype(jnp.float32))]
    reduce_sum x2 -> x0, other arithmetic: 5 us -> none  [the longest x1 2.99 us: together(): jnp.sum(total * scale, 0)]
    reduce_max x2 -> x0, other arithmetic: 2.43 us -> none  [the longest x1 2.29 us: together(): scale = jnp.exp(high - jnp.max(high, 0))]
    unnamed x0 -> x1, local copies, waits for them, and re-layouts: none -> 1.57 us
    mul x1 -> x0, local copies, waits for them, and re-layouts: 1.56 us -> none  [together(): seen * scale]
  transfers between devices with their start and end apart: 1 -> 0, of which waited for: 1 -> 0; matrix products, arithmetic and copies ran while one was open for 0% -> 0% of each run, Pallas kernels for 0% -> 0%
where the time goes in v1:
time: 39 us; the launch traced here: 38.9 us
  Pallas kernels  37.3 us (96%)
  local copies, waits for them, and re-layouts  1.57 us (4%)
    pallas_call x1, Pallas kernels, attend(): pl.pallas_call(functools.partial(kernel, axis, devices, rounds), out_shap...  37.3 us
    unnamed x1, local copies, waits for them, and re-layouts  1.57 us

profile of v1, /device:TPU:21, one launch (start us, length us, event | category | flops | bytes accessed | tf_op | source)
XLA Modules:
  0.0 38.9 jit_solution(14614472140756577479)
XLA Ops:
  0.0 37.3 %attend.1 = bf16[32,16,128]{2,1,0:T(8,128)(2,1)} custom-call(bf16[32,16,128]{2,1,0:T(8,128)(2,1)} %q_hbm.1, bf16[32,2,2048,128]{3,2,1,0:T(8,128)(2,1)} %bitcast.2, bf16[32,2,2048,128]{3,2,1,0:T(8,128)(2,1)} %bitcast.3), custom_call_target="tpu_custom_call" | custom-call | tf_op jit(solution)/shard_map/attend/pallas_call | solution.py:246
  37.3 1.6 %copy.5 = bf16[32,16,128]{2,1,0:T(8,128)(2,1)} copy(bf16[32,16,128]{2,1,0:T(8,128)(2,1)} %attend.1) | data formatting | bytes 262144

commit v2 on v1

v2 whole, which is shorter than its diff:
```python
import functools

import jax
import jax.numpy as jnp
from jax import lax
from jax.experimental import pallas as pl
from jax.experimental.pallas import tpu as pltpu
from jax.sharding import PartitionSpec as P

LOG2E = 1.4426950408889634
SLOTS = 12
LANES = 128
DIRECT = 4
EARLY = 4
LAG = 9
MESH = pl.DeviceIdType.MESH


def kernel(axis, devices, shared, q_hbm, k_hbm, v_hbm, o_ref, *scratch):
    (qbuf, kbuf, vbuf, sbuf, hbuf, pbuf, part, stat, rpart, rstat, tpart, tstat, cols, obuf,
     qsem, ksem, vsem, psend, precv, ssend, srecv, tpsend, tprecv, tssend, tsrecv, gsend, grecv) = scratch
    n, heads, head = q_hbm.shape
    half = k_hbm.shape[2]
    chunks = half // LANES
    me = lax.axis_index(axis)
    others = sorted(range(1, devices), key=lambda d: -min(d, devices - d))
    factor = head ** -0.5 * LOG2E

    def peer(d):
        return lax.rem(me + d, devices)

    def to(src, dst, send, recv, device):
        return pltpu.make_async_remote_copy(src, dst, send, recv, device_id={axis: device}, device_id_type=MESH)

    def await_bytes(ref, sem):
        pltpu.make_async_copy(ref, ref, sem).wait()

    def kcopy(i):
        return pltpu.make_async_copy(k_hbm.at[i], kbuf.at[lax.rem(i, SLOTS)], ksem.at[lax.rem(i, SLOTS)])

    def vcopy(i):
        return pltpu.make_async_copy(v_hbm.at[i], vbuf.at[lax.rem(i, SLOTS)], vsem.at[lax.rem(i, SLOTS)])

    row = lax.broadcasted_iota(jnp.int32, (2 * heads, LANES), 0)
    lane = lax.broadcasted_iota(jnp.int32, (2 * heads, LANES), 1)
    keep = lax.rem(row, heads) == lax.rem(lane, heads)
    own = keep[:heads]
    first = row[:heads] == lane[:heads]

    def scores(i):
        q = qbuf[i]
        z = jnp.zeros_like(q)
        qq = jnp.concatenate([jnp.concatenate([q, z], 1), jnp.concatenate([z, q], 1)], 0)
        slot = lax.rem(i, SLOTS)
        kk = jnp.concatenate([kbuf[slot, 0], kbuf[slot, 1]], 1)
        s = lax.dot_general(qq, kk, (((1,), (1,)), ((), ())), preferred_element_type=jnp.float32)
        cs = [jnp.where(keep, s[:, c * LANES:(c + 1) * LANES], -jnp.inf) for c in range(chunks)]
        high = functools.reduce(jnp.maximum, cs)
        return cs, jnp.maximum(high[:heads], high[heads:])

    def put_scores(t, cs, high):
        for c in range(chunks):
            sbuf[t, :, c * LANES:(c + 1) * LANES] = cs[c]
        hbuf[t] = high

    def weigh(t):
        high = jnp.max(hbuf[t], 1, keepdims=True) * factor
        both = jnp.broadcast_to(jnp.concatenate([high, high], 0), (2 * heads, LANES))
        ps = [jnp.exp2(sbuf[t, :, c * LANES:(c + 1) * LANES] * factor - both) for c in range(chunks)]
        total = functools.reduce(jnp.add, ps)
        total = jnp.sum(total[:heads] + total[heads:], 1, keepdims=True)
        as_row = lambda x: jnp.sum(jnp.where(own, jnp.broadcast_to(x, (heads, LANES)), 0.0), 0, keepdims=True)
        return [p.astype(jnp.bfloat16) for p in ps], jnp.concatenate([as_row(high), as_row(total)], 0)

    def put_weights(t, ps):
        for c in range(chunks):
            pbuf[t, :, c * LANES:(c + 1) * LANES] = ps[c]

    def seen(t, i):
        slot = lax.rem(i, SLOTS)
        vv = jnp.concatenate([vbuf[slot, 0], vbuf[slot, 1]], 1)
        o = sum(jnp.dot(pbuf[t, :, x:x + half // 2], vv[x:x + half // 2], preferred_element_type=jnp.float32) for x in (0, half // 2))
        return (o[:heads, :head] + o[heads:, head:]).astype(jnp.bfloat16)

    def steps(i, put_stat, put_part, put_next):
        for u in range(2):
            kcopy(i + 2 + u).wait()
            vcopy(i + u).wait()
        for u in range(2):
            cs, high = scores(i + 2 + u)
            ps, st = weigh(1 - u)
            put_part(i + u, seen(u, i + u))
            (put_next if u else put_stat)(i + 1 + u, st)
            put_scores(u, cs, high)
            put_weights(1 - u, ps)

        for u in range(2):
            @pl.when(i + u + 2 + SLOTS < n)
            def _():
                kcopy(i + u + 2 + SLOTS).start()

            @pl.when(i + u + SLOTS < n)
            def _():
                vcopy(i + u + SLOTS).start()

    def put_stat(i, st):
        stat[i] = st

    def put_part(i, x):
        part[i] = x

    def put_tail_stat(i, st):
        tstat[i - shared, me] = st

    def put_tail_part(i, x):
        tpart[i - shared, me] = x

    def send_owner(i):
        owner, g = lax.rem(i, devices), lax.div(i, devices)

        @pl.when(owner != me)
        def _():
            to(stat.at[i], rstat.at[g, me], ssend.at[i], srecv.at[g], owner).start()
            to(part.at[i], rpart.at[g, me], psend.at[i], precv.at[g], owner).start()

    def shares(st):
        high, total = st[:, 0, :], st[:, 1, :]
        e = jnp.exp2(high - jnp.max(high, 0, keepdims=True))
        w = e / jnp.sum(e * total, 0, keepdims=True)
        return [jnp.sum(jnp.where(first, jnp.broadcast_to(w[d:d + 1], (heads, LANES)), 0.0), 1, keepdims=True) for d in range(devices)]

    def join(i):
        g = lax.div(i, devices)
        rstat[g, me] = stat[i]
        rpart[g, me] = part[i]
        await_bytes(rstat.at[g, pl.ds(0, devices - 1)], srecv.at[g])
        await_bytes(rpart.at[g, pl.ds(0, devices - 1)], precv.at[g])
        w = shares(rstat[g])
        obuf[i] = functools.reduce(jnp.add, [rpart[g, d].astype(jnp.float32) * w[d] for d in range(devices)]).astype(jnp.bfloat16)
        for d in others:
            to(obuf.at[i], obuf.at[i], gsend.at[g], grecv.at[i], peer(d)).start()

    def send_tail_stat(i):
        t = i - shared
        for d in others:
            to(tstat.at[t, me], tstat.at[t, me], tssend.at[t], tsrecv.at[t], peer(d)).start()

    def send_tail_part(i):
        t = i - shared
        for d in others:
            to(tpart.at[t, me], tpart.at[t, me], tpsend.at[t], tprecv.at[t], peer(d)).start()

    qcopy = pltpu.make_async_copy(q_hbm, qbuf, qsem)
    qcopy.start()
    kcopy(0).start()
    kcopy(1).start()

    @pl.loop(0, SLOTS - 2)
    def _(i):
        kcopy(i + 2).start()
        vcopy(i).start()

    vcopy(SLOTS - 2).start()
    vcopy(SLOTS - 1).start()
    barrier = pltpu.get_barrier_semaphore()
    for d in others:
        pl.semaphore_signal(barrier, inc=1, device_id={axis: peer(d)}, device_id_type=MESH)
    qcopy.wait()
    kcopy(0).wait()
    put_scores(0, *scores(0))
    kcopy(1).wait()
    cs, high = scores(1)
    ps, st = weigh(0)
    put_stat(0, st)
    put_scores(1, cs, high)
    put_weights(0, ps)
    kcopy(SLOTS).start()
    kcopy(SLOTS + 1).start()

    @pl.loop(0, EARLY, step=2)
    def _(i):
        steps(i, put_stat, put_part, put_stat)

    pl.semaphore_wait(barrier, devices - 1)

    @pl.loop(0, EARLY)
    def _(i):
        send_owner(i)

    def joint(i):
        send_owner(i)

        @pl.when(jnp.logical_and(i >= LAG, lax.rem(i - LAG + devices, devices) == me))
        def _():
            join(i - LAG)

    @pl.loop(EARLY, shared - 2, step=2)
    def _(i):
        steps(i, put_stat, put_part, put_stat)
        joint(i)
        joint(i + 1)

    steps(shared - 2, put_stat, put_part, put_tail_stat)
    joint(shared - 2)
    joint(shared - 1)
    send_tail_stat(shared)

    def late_join(i):
        @pl.when(jnp.logical_and(lax.rem(i - LAG, devices) == me, i - LAG < shared))
        def _():
            join(i - LAG)

    @pl.loop(shared, n - 2, step=2)
    def _(i):
        steps(i, put_tail_stat, put_tail_part, put_tail_stat)
        for u in range(2):
            send_tail_part(i + u)
            send_tail_stat(i + 1 + u)
        late_join(i)
        late_join(i + 1)

    vcopy(n - 2).wait()
    ps, st = weigh(1)
    put_tail_stat(n - 1, st)
    put_tail_part(n - 2, seen(0, n - 2))
    put_weights(1, ps)
    send_tail_stat(n - 1)
    send_tail_part(n - 2)
    vcopy(n - 1).wait()
    put_tail_part(n - 1, seen(1, n - 1))
    send_tail_part(n - 1)
    late_join(n - 2)

    @pl.loop(n - 1, shared + LAG)
    def _(i):
        late_join(i)

    @pl.loop(0, n - shared)
    def _(t):
        await_bytes(tstat.at[t, pl.ds(0, devices - 1)], tsrecv.at[t])
        w = shares(tstat[t])
        for d in range(devices):
            cols[t, d] = jnp.broadcast_to(w[d], (heads, head))

    @pl.loop(0, n - shared)
    def _(t):
        await_bytes(tpart.at[t, pl.ds(0, devices - 1)], tprecv.at[t])
        o_ref[shared + t] = functools.reduce(
            jnp.add, [tpart[t, d].astype(jnp.float32) * cols[t, d] for d in range(devices)]
        ).astype(jnp.bfloat16)

    @pl.loop(0, shared)
    def _(i):
        mine = lax.rem(i, devices) == me

        @pl.when(jnp.logical_not(mine))
        def _():
            await_bytes(obuf.at[i], grecv.at[i])

        o_ref[i] = obuf[i]

    @pl.loop(0, shared)
    def _(i):
        mine = lax.rem(i, devices) == me

        @pl.when(mine)
        def _():
            await_bytes(obuf.at[pl.ds(0, devices - 1)], gsend.at[lax.div(i, devices)])

        @pl.when(jnp.logical_not(mine))
        def _():
            await_bytes(stat.at[i], ssend.at[i])
            await_bytes(part.at[i], psend.at[i])

    @pl.loop(0, n - shared)
    def _(t):
        await_bytes(tstat.at[t, pl.ds(0, devices - 1)], tssend.at[t])
        await_bytes(tpart.at[t, pl.ds(0, devices - 1)], tpsend.at[t])


def attend(axis, devices, q, k, v):
    n, tokens, heads, head = k.shape
    half = tokens * heads // 2
    k = k.reshape(n, 2, half, head)
    v = v.reshape(n, 2, half, head)
    tail = DIRECT
    shared = n - tail
    rounds = -(-shared // devices)
    dma = pltpu.SemaphoreType.DMA
    bf16, f32 = jnp.bfloat16, jnp.float32
    return pl.pallas_call(
        functools.partial(kernel, axis, devices, shared),
        out_shape=pltpu.VMEM((n, heads, head), bf16),
        in_specs=[pl.BlockSpec(memory_space=pl.ANY)] * 3,
        out_specs=pl.BlockSpec(memory_space=pltpu.VMEM),
        scratch_shapes=[
            pltpu.VMEM((n, heads, head), bf16),
            pltpu.VMEM((SLOTS, 2, half, head), bf16),
            pltpu.VMEM((SLOTS, 2, half, head), bf16),
            pltpu.VMEM((2, 2 * heads, half), f32),
            pltpu.VMEM((2, heads, LANES), f32),
            pltpu.VMEM((2, 2 * heads, half), bf16),
            pltpu.VMEM((shared, heads, head), bf16),
            pltpu.VMEM((shared, 2, LANES), f32),
            pltpu.VMEM((rounds, devices, heads, head), bf16),
            pltpu.VMEM((rounds, devices, 2, LANES), f32),
            pltpu.VMEM((tail, devices, heads, head), bf16),
            pltpu.VMEM((tail, devices, 2, LANES), f32),
            pltpu.VMEM((tail, devices, heads, head), f32),
            pltpu.VMEM((shared, heads, head), bf16),
            dma, dma((SLOTS,)), dma((SLOTS,)),
            dma((shared,)), dma((rounds,)), dma((shared,)), dma((rounds,)),
            dma((tail,)), dma((tail,)), dma((tail,)), dma((tail,)),
            dma((rounds,)), dma((shared,)),
        ],
        compiler_params=pltpu.CompilerParams(collective_id=0, has_side_effects=True, vmem_limit_bytes=56 << 20),
        name="attend",
    )(q, k, v)


def solution(mesh):
    def step(q, k, v):
        return attend("sp", mesh.shape["sp"], q, k, v)

    return jax.shard_map(
        step,
        mesh=mesh,
        in_specs=(P("dp", None, None), P("dp", "sp", None, None), P("dp", "sp", None, None)),
        out_specs=P("dp", None, None),
        check_vma=False,
    )
```

time: 39 us -> 36.2 us (0.928)
  Pallas kernels: 37.3 us -> 35.3 us
  local copies, waits for them, and re-layouts: 1.57 us -> 0.66 us
    pallas_call x1, Pallas kernels: 37.3 us -> 35.3 us  [attend(): pl.pallas_call(functools.partial(kernel, axis, devices, shared), out_shap...]
    unnamed x1, local copies, waits for them, and re-layouts: 1.57 us -> 0.66 us
where the time goes in v2:
time: 36.2 us; the launch traced here: 35.9 us
  Pallas kernels  35.3 us (98%)
  local copies, waits for them, and re-layouts  0.66 us (2%)
    pallas_call x1, Pallas kernels, attend(): pl.pallas_call(functools.partial(kernel, axis, devices, shared), out_shap...  35.3 us

profile of v2, /device:TPU:21, one launch (start us, length us, event | category | flops | bytes accessed | tf_op | source)
XLA Modules:
  0.0 35.9 jit_solution(17867252602843865739)
XLA Ops:
  0.0 35.3 %attend.1 = bf16[32,16,128]{2,1,0:T(8,128)(2,1)S(1)} custom-call(bf16[32,16,128]{2,1,0:T(8,128)(2,1)} %q_hbm.1, bf16[32,2,2048,128]{3,2,1,0:T(8,128)(2,1)} %bitcast.2, bf16[32,2,2048,128]{3,2,1,0:T(8,128)(2,1)} %bitcast.3), custom_call_target="tpu_custom_call" | custom-call | tf_op jit(solution)/shard_map/attend/pallas_call | solution.py:291
  35.3 0.7 %copy.5 = bf16[32,16,128]{2,1,0:T(8,128)(2,1)} copy(bf16[32,16,128]{2,1,0:T(8,128)(2,1)S(1)} %attend.1) | data formatting | bytes 262144

commit v3 on v2

--- a/solution.py
+++ b/solution.py
@@ -10,14 +10,15 @@
 LOG2E = 1.4426950408889634
 SLOTS = 12
 LANES = 128
-DIRECT = 4
+DIRECT = 2
 EARLY = 4
-LAG = 9
+OWNERS = (2, 1, 5, 0, 6, 7, 3, 4)
+LAG = 14
 MESH = pl.DeviceIdType.MESH
 
 
 def kernel(axis, devices, shared, q_hbm, k_hbm, v_hbm, o_ref, *scratch):
-    (qbuf, kbuf, vbuf, sbuf, hbuf, pbuf, part, stat, rpart, rstat, tpart, tstat, cols, obuf,
+    (qbuf, kbuf, vbuf, sbuf, hbuf, pbuf, part, stat, rpart, rstat, tpart, tstat, cols,
      qsem, ksem, vsem, psend, precv, ssend, srecv, tpsend, tprecv, tssend, tsrecv, gsend, grecv) = scratch
     n, heads, head = q_hbm.shape
     half = k_hbm.shape[2]
@@ -25,6 +26,9 @@
     me = lax.axis_index(axis)
     others = sorted(range(1, devices), key=lambda d: -min(d, devices - d))
     factor = head ** -0.5 * LOG2E
+
+    pick = lambda table, x: sum(jnp.where(x == j, y, 0) for j, y in enumerate(table))
+    place = pick([OWNERS.index(d) for d in range(devices)], me)
 
     def peer(d):
         return lax.rem(me + d, devices)
@@ -116,7 +120,7 @@
         tpart[i - shared, me] = x
 
     def send_owner(i):
-        owner, g = lax.rem(i, devices), lax.div(i, devices)
+        owner, g = pick(OWNERS, lax.rem(i, devices)), lax.div(i, devices)
 
         @pl.when(owner != me)
         def _():
@@ -136,9 +140,9 @@
         await_bytes(rstat.at[g, pl.ds(0, devices - 1)], srecv.at[g])
         await_bytes(rpart.at[g, pl.ds(0, devices - 1)], precv.at[g])
         w = shares(rstat[g])
-        obuf[i] = functools.reduce(jnp.add, [rpart[g, d].astype(jnp.float32) * w[d] for d in range(devices)]).astype(jnp.bfloat16)
+        o_ref[i] = functools.reduce(jnp.add, [rpart[g, d].astype(jnp.float32) * w[d] for d in range(devices)]).astype(jnp.bfloat16)
         for d in others:
-            to(obuf.at[i], obuf.at[i], gsend.at[g], grecv.at[i], peer(d)).start()
+            to(o_ref.at[i], o_ref.at[i], gsend.at[g], grecv.at[i], peer(d)).start()
 
     def send_tail_stat(i):
         t = i - shared
@@ -190,7 +194,7 @@
     def joint(i):
         send_owner(i)
 
-        @pl.when(jnp.logical_and(i >= LAG, lax.rem(i - LAG + devices, devices) == me))
+        @pl.when(jnp.logical_and(i >= LAG, lax.rem(i - LAG + devices, devices) == place))
         def _():
             join(i - LAG)
 
@@ -206,7 +210,7 @@
     send_tail_stat(shared)
 
     def late_join(i):
-        @pl.when(jnp.logical_and(lax.rem(i - LAG, devices) == me, i - LAG < shared))
+        @pl.when(jnp.logical_and(lax.rem(i - LAG, devices) == place, i - LAG < shared))
         def _():
             join(i - LAG)
 
@@ -242,40 +246,33 @@
         for d in range(devices):
             cols[t, d] = jnp.broadcast_to(w[d], (heads, head))
 
+    def settle(i):
+        @pl.when(lax.rem(i, devices) == place)
+        def _():
+            await_bytes(o_ref.at[pl.ds(0, devices - 1)], gsend.at[lax.div(i, devices)])
+
+        @pl.when(lax.rem(i, devices) != place)
+        def _():
+            await_bytes(stat.at[i], ssend.at[i])
+            await_bytes(part.at[i], psend.at[i])
+            await_bytes(o_ref.at[i], grecv.at[i])
+
+    @pl.loop(0, shared - devices)
+    def _(i):
+        settle(i)
+
     @pl.loop(0, n - shared)
     def _(t):
         await_bytes(tpart.at[t, pl.ds(0, devices - 1)], tprecv.at[t])
         o_ref[shared + t] = functools.reduce(
             jnp.add, [tpart[t, d].astype(jnp.float32) * cols[t, d] for d in range(devices)]
         ).astype(jnp.bfloat16)
-
-    @pl.loop(0, shared)
-    def _(i):
-        mine = lax.rem(i, devices) == me
-
-        @pl.when(jnp.logical_not(mine))
-        def _():
-            await_bytes(obuf.at[i], grecv.at[i])
-
-        o_ref[i] = obuf[i]
-
-    @pl.loop(0, shared)
-    def _(i):
-        mine = lax.rem(i, devices) == me
-
-        @pl.when(mine)
-        def _():
-            await_bytes(obuf.at[pl.ds(0, devices - 1)], gsend.at[lax.div(i, devices)])
-
-        @pl.when(jnp.logical_not(mine))
-        def _():
-            await_bytes(stat.at[i], ssend.at[i])
-            await_bytes(part.at[i], psend.at[i])
-
-    @pl.loop(0, n - shared)
-    def _(t):
         await_bytes(tstat.at[t, pl.ds(0, devices - 1)], tssend.at[t])
         await_bytes(tpart.at[t, pl.ds(0, devices - 1)], tpsend.at[t])
+
+    @pl.loop(shared - devices, shared)
+    def _(i):
+        settle(i)
 
 
 def attend(axis, devices, q, k, v):
@@ -307,7 +304,6 @@
             pltpu.VMEM((tail, devices, heads, head), bf16),
             pltpu.VMEM((tail, devices, 2, LANES), f32),
             pltpu.VMEM((tail, devices, heads, head), f32),
-            pltpu.VMEM((shared, heads, head), bf16),
             dma, dma((SLOTS,)), dma((SLOTS,)),
             dma((shared,)), dma((rounds,)), dma((shared,)), dma((rounds,)),
             dma((tail,)), dma((tail,)), dma((tail,)), dma((tail,)),

time: 36.2 us -> 35.9 us (level)
  no operation moved by 1% of the time
where the time goes in v3:
time: 35.9 us; the launch traced here: 35.8 us
  Pallas kernels  35.2 us (98%)
  local copies, waits for them, and re-layouts  0.66 us (2%)
    pallas_call x1, Pallas kernels, attend(): pl.pallas_call(functools.partial(kernel, axis, devices, shared), out_shap...  35.2 us

profile of v3, /device:TPU:21, one launch (start us, length us, event | category | flops | bytes accessed | tf_op | source)
XLA Modules:
  0.0 35.8 jit_solution(6456066636361510856)
XLA Ops:
  0.0 35.2 %attend.1 = bf16[32,16,128]{2,1,0:T(8,128)(2,1)S(1)} custom-call(bf16[32,16,128]{2,1,0:T(8,128)(2,1)} %q_hbm.1, bf16[32,2,2048,128]{3,2,1,0:T(8,128)(2,1)} %bitcast.2, bf16[32,2,2048,128]{3,2,1,0:T(8,128)(2,1)} %bitcast.3), custom_call_target="tpu_custom_call" | custom-call | tf_op jit(solution)/shard_map/attend/pallas_call | solution.py:288
  35.2 0.7 %copy.5 = bf16[32,16,128]{2,1,0:T(8,128)(2,1)} copy(bf16[32,16,128]{2,1,0:T(8,128)(2,1)S(1)} %attend.1) | data formatting | bytes 262144

commit v4 on v3

--- a/solution.py
+++ b/solution.py
@@ -24,14 +24,14 @@
     half = k_hbm.shape[2]
     chunks = half // LANES
     me = lax.axis_index(axis)
-    others = sorted(range(1, devices), key=lambda d: -min(d, devices - d))
+    others = range(devices - 1)
     factor = head ** -0.5 * LOG2E
 
     pick = lambda table, x: sum(jnp.where(x == j, y, 0) for j, y in enumerate(table))
     place = pick([OWNERS.index(d) for d in range(devices)], me)
 
     def peer(d):
-        return lax.rem(me + d, devices)
+        return jnp.where(d >= me, d + 1, d)
 
     def to(src, dst, send, recv, device):
         return pltpu.make_async_remote_copy(src, dst, send, recv, device_id={axis: device}, device_id_type=MESH)

time: 35.9 us -> 35.6 us (level)
  no operation moved by 1% of the time
where the time goes in v4:
time: 35.6 us; the launch traced here: 35.5 us
  Pallas kernels  34.9 us (98%)
  local copies, waits for them, and re-layouts  0.66 us (2%)
    pallas_call x1, Pallas kernels, attend(): pl.pallas_call(functools.partial(kernel, axis, devices, shared), out_shap...  34.9 us

profile of v4, /device:TPU:21, one launch (start us, length us, event | category | flops | bytes accessed | tf_op | source)
XLA Modules:
  0.0 35.5 jit_solution(14243895961744558448)
XLA Ops:
  0.0 34.9 %attend.1 = bf16[32,16,128]{2,1,0:T(8,128)(2,1)S(1)} custom-call(bf16[32,16,128]{2,1,0:T(8,128)(2,1)} %q_hbm.1, bf16[32,2,2048,128]{3,2,1,0:T(8,128)(2,1)} %bitcast.2, bf16[32,2,2048,128]{3,2,1,0:T(8,128)(2,1)} %bitcast.3), custom_call_target="tpu_custom_call" | custom-call | tf_op jit(solution)/shard_map/attend/pallas_call | solution.py:288
  34.9 0.7 %copy.5 = bf16[32,16,128]{2,1,0:T(8,128)(2,1)} copy(bf16[32,16,128]{2,1,0:T(8,128)(2,1)S(1)} %attend.1) | data formatting | bytes 262144
